TPU v7x, 32 devices: a 4x4x1 block of a 4x4x8 slice. The times are simulated.
32 devices in a mesh: dp: 1 (over z), tp: 4 (over y), fsdp: 8 (over x, core).
Axes of the slice: x: 4, y: 4, z: 1, core: 2. Of those that a mesh axis runs over, the one named last changes fastest.
The devices are a block of a 4x4x8 slice.
Arguments:
- x: bfloat16 [8, 512, 4096], P(('dp', 'fsdp'))
- w_query: bfloat16 [2, 4096, 4096], P(None, 'fsdp', 'tp')
- w_key: bfloat16 [2, 4096, 4096], P(None, 'fsdp', 'tp')
- w_value: bfloat16 [2, 4096, 4096], P(None, 'fsdp', 'tp')
- w_out: bfloat16 [2, 4096, 4096], P(None, 'tp', 'fsdp')
- w_gate: bfloat16 [2, 4096, 11008], P(None, 'fsdp', 'tp')
- w_up: bfloat16 [2, 4096, 11008], P(None, 'fsdp', 'tp')
- w_down: bfloat16 [2, 11008, 4096], P(None, 'tp', 'fsdp')
- q_norm_w: float32 [2, 4096], P(None, 'tp')
- k_norm_w: float32 [2, 4096], P(None, 'tp')
- attn_norm_w: float32 [2, 4096], P(None, 'fsdp')
- ffn_norm_w: float32 [2, 4096], P(None, 'fsdp')
Outputs:
- output 1: bfloat16 [8, 512, 4096], P(('dp', 'fsdp'))
- output 2: bfloat16 [2, 8, 512, 32, 128], P(None, ('dp', 'fsdp'), None, 'tp')
- output 3: bfloat16 [2, 8, 512, 32, 128], P(None, ('dp', 'fsdp'), None, 'tp')
All inputs are finite; a program needn't handle non-finite values.
Results may differ from a plain program's by a relative error of at most 0.02.
Values are sent between devices in bfloat16 or wider.
A program may use at most 768 MiB of HBM per device.

v0:
```python
import jax
import jax.numpy as jnp
from jax import lax
from jax.sharding import PartitionSpec as P

HEAD_DIM = 128
NORM_EPS = 1e-6
ROPE_THETA = 500000.0


def rope_tables(seq_len):
    half = HEAD_DIM // 2
    inv_freq = ROPE_THETA ** (-2.0 * jnp.arange(half, dtype=jnp.float32) / HEAD_DIM)
    angles = jnp.arange(seq_len, dtype=jnp.float32)[:, None] * inv_freq[None, :]
    return jnp.cos(angles)[:, None, :], jnp.sin(angles)[:, None, :]


def apply_rope(vals, cos_t, sin_t):
    half = HEAD_DIM // 2
    first = vals[..., :half]
    second = vals[..., half:]
    return jnp.concatenate([first * cos_t - second * sin_t, second * cos_t + first * sin_t], axis=-1)


def rms_scale(vals):
    return lax.rsqrt(jnp.mean(vals * vals, axis=-1, keepdims=True) + NORM_EPS)


def attend(queries, keys_rot, values, causal):
    scores = jnp.einsum('bqhd,bkhd->bhqk', queries, keys_rot, preferred_element_type=jnp.float32) * (HEAD_DIM ** -0.5)
    scores = jnp.where(causal, scores, -jnp.inf)
    attn_probs = jax.nn.softmax(scores, axis=-1).astype(jnp.bfloat16)
    return jnp.einsum('bhqk,bkhd->bqhd', attn_probs, values, preferred_element_type=jnp.float32).astype(jnp.bfloat16)


def solution(mesh):
    batch_axes = ('dp', 'fsdp')
    act_spec = P(batch_axes, None, None)
    in_cols = P(None, 'fsdp', 'tp')
    in_rows = P(None, 'tp', 'fsdp')
    tp_gain = P(None, 'tp')
    fsdp_gain = P(None, 'fsdp')
    cache_spec = P(None, batch_axes, None, 'tp', None)

    def local_layers(x, w_query, w_key, w_value, w_out, w_gate, w_up, w_down, q_norm_w, k_norm_w, attn_norm_w, ffn_norm_w):
        batch, seq_len, width = x.shape
        tokens = batch * seq_len
        head_shape = (batch, seq_len, w_query.shape[2] // HEAD_DIM, HEAD_DIM)
        cos_t, sin_t = rope_tables(seq_len)
        causal = jnp.arange(seq_len)[:, None] >= jnp.arange(seq_len)[None, :]
        hidden = x.reshape(tokens, width)
        k_layers = []
        v_layers = []
        for layer in range(w_query.shape[0]):
            wq_full = lax.all_gather(w_query[layer], 'fsdp', axis=0, tiled=True)
            wk_full = lax.all_gather(w_key[layer], 'fsdp', axis=0, tiled=True)
            wv_full = lax.all_gather(w_value[layer], 'fsdp', axis=0, tiled=True)
            q_raw = jnp.dot(hidden, wq_full, preferred_element_type=jnp.float32)
            k_raw = jnp.dot(hidden, wk_full, preferred_element_type=jnp.float32)
            values = jnp.dot(hidden, wv_full, preferred_element_type=jnp.float32).astype(jnp.bfloat16).reshape(head_shape)
            sq_local = jnp.stack([jnp.sum(q_raw * q_raw, axis=-1), jnp.sum(k_raw * k_raw, axis=-1)])
            sq_total = lax.psum(sq_local, 'tp')
            inv_rms = lax.rsqrt(sq_total / width + NORM_EPS)
            queries = apply_rope((q_raw * inv_rms[0][:, None] * q_norm_w[layer]).reshape(head_shape), cos_t, sin_t).astype(jnp.bfloat16)
            keys_rot = apply_rope((k_raw * inv_rms[1][:, None] * k_norm_w[layer]).reshape(head_shape), cos_t, sin_t).astype(jnp.bfloat16)
            attended = attend(queries, keys_rot, values, causal)
            wo_full = lax.all_gather(w_out[layer], 'fsdp', axis=1, tiled=True)
            a_part = jnp.dot(attended.reshape(tokens, -1), wo_full, preferred_element_type=jnp.float32).astype(jnp.bfloat16)
            a_out = lax.psum(a_part, 'tp').astype(jnp.float32)
            attn_gain = lax.all_gather(attn_norm_w[layer], 'fsdp', axis=0, tiled=True)
            h_new = (hidden.astype(jnp.float32) + a_out * rms_scale(a_out) * attn_gain).astype(jnp.bfloat16)
            wg_full = lax.all_gather(w_gate[layer], 'fsdp', axis=0, tiled=True)
            wu_full = lax.all_gather(w_up[layer], 'fsdp', axis=0, tiled=True)
            gate = jnp.dot(h_new, wg_full, preferred_element_type=jnp.float32)
            up_val = jnp.dot(h_new, wu_full, preferred_element_type=jnp.float32)
            hidden_act = (jax.nn.silu(gate) * up_val).astype(jnp.bfloat16)
            wd_full = lax.all_gather(w_down[layer], 'fsdp', axis=1, tiled=True)
            m_part = jnp.dot(hidden_act, wd_full, preferred_element_type=jnp.float32).astype(jnp.bfloat16)
            m_out = lax.psum(m_part, 'tp').astype(jnp.float32)
            ffn_gain = lax.all_gather(ffn_norm_w[layer], 'fsdp', axis=0, tiled=True)
            hidden = (h_new.astype(jnp.float32) + m_out * rms_scale(m_out) * ffn_gain).astype(jnp.bfloat16)
            k_layers.append(keys_rot)
            v_layers.append(values)
        return hidden.reshape(batch, seq_len, width), jnp.stack(k_layers), jnp.stack(v_layers)

    return jax.shard_map(local_layers, mesh=mesh,
                         in_specs=(act_spec, in_cols, in_cols, in_cols, in_rows, in_cols, in_cols, in_rows,
                                   tp_gain, tp_gain, fsdp_gain, fsdp_gain),
                         out_specs=(act_spec, cache_spec, cache_spec), check_vma=False)
```

profile of v0, /device:TPU:97, one launch (start us, length us, event | category | flops | bytes accessed | tf_op | source)
XLA Modules:
  0.0 1484.8 jit_solution(14004979567917540810)
XLA Ops:
  20.8 41.1 %all-gather.35.cloned.1.call-done = bf16[1,4096,1024]{2,1,0:T(8,128)(2,1)} async-done(((bf16[1,512,1024]{2,1,0:T(8,128)(2,1)}), bf16[1,4096,1024]{2,1,0:T(8,128)(2,1)}) %all-gather.35.cloned.1.call-update) | async-done | bytes 8388624 | tf_op jit(solution)/shard_map/all_gather | solution.py:55
  61.9 8.3 multiply_reduce_fusion.3
  70.2 41.1 %all-gather.37.cloned.1.call-done = bf16[1,4096,1024]{2,1,0:T(8,128)(2,1)} async-done(((bf16[1,512,1024]{2,1,0:T(8,128)(2,1)}), bf16[1,4096,1024]{2,1,0:T(8,128)(2,1)}) %all-gather.37.cloned.1.call-update) | async-done | bytes 8388624 | tf_op jit(solution)/shard_map/all_gather | solution.py:56
  111.3 10.5 multiply_reduce_fusion.2
  121.8 9.3 psum.42
  134.8 26.0 %all-gather.33.cloned.1.call-done = bf16[1,4096,1024]{2,1,0:T(8,128)(2,1)} async-done(((bf16[1,512,1024]{2,1,0:T(8,128)(2,1)}), bf16[1,4096,1024]{2,1,0:T(8,128)(2,1)}) %all-gather.33.cloned.1.call-update) | async-done | bytes 8388624 | tf_op jit(solution)/shard_map/all_gather | solution.py:57
  160.7 9.1 fusion.76
  179.7 5.5 fusion.135
  185.2 4.1 fusion.85
  189.3 20.2 %all-gather.39.cloned.1.call-done = bf16[1,1024,4096]{2,1,0:T(8,128)(2,1)} async-done(((bf16[1,1024,512]{2,1,0:T(8,128)(2,1)}), bf16[1,1024,4096]{2,1,0:T(8,128)(2,1)}) %all-gather.39.cloned.1.call-update) | async-done | bytes 8388624 | tf_op jit(solution)/shard_map/all_gather | solution.py:67
  209.4 9.5 fusion.54
  219.1 5.5 fusion.119
  224.7 5.4 fusion.118
  230.3 5.4 fusion.120
  236.4 18.1 %all-gather.4 = f32[1,4096]{1,0:T(1,128)S(1)} all-gather(f32[1,512]{1,0:T(1,128)S(1)} %get-tuple-element.50), channel_id=6, replica_groups=mesh['dp'=1,'tp'=4,'fsdp'=8] {'fsdp'}, dimensions={1}, use_global_device_ids=true | all-gather | bytes 18432 | tf_op jit(solution)/shard_map/all_gather | solution.py:70
  254.5 51.8 %all-reduce.5.cloned.1.call-done = bf16[512,4096]{1,0:T(8,128)(2,1)} async-done(((bf16[512,4096]{1,0:T(8,128)(2,1)}), bf16[512,4096]{1,0:T(8,128)(2,1)}) %all-reduce.5.cloned.1.call-update) | async-done | bytes 4194320 | tf_op jit(solution)/shard_map/psum | solution.py:69
  309.7 6.4 fusion.17
  316.1 99.2 %all-gather.41.cloned.1.call-done = bf16[1,4096,2752]{1,2,0:T(8,128)(2,1)} async-done(((bf16[1,512,2752]{1,2,0:T(8,128)(2,1)}), bf16[1,4096,2752]{1,2,0:T(8,128)(2,1)}) %all-gather.41.cloned.1.call-update) | async-done | bytes 22544400 | tf_op jit(solution)/shard_map/all_gather | solution.py:72
  415.3 19.3 %fusion.12 = f32[512,2752]{0,1:T(8,128)} fusion(bf16[512,4096]{1,0:T(8,128)(2,1)} %fusion.17, bf16[1,4096,2752]{1,2,0:T(8,128)(2,1)} %all-gather.41.cloned.1.call-done), kind=kOutput, calls=%fused_computation.12 | convolution fusion | flops 11542724608 | bytes 32374784 | tf_op jit(solution)/shard_map/dot_general | solution.py:74
  434.6 90.3 %all-gather.43.cloned.1.call-done = bf16[1,4096,2752]{1,2,0:T(8,128)(2,1)} async-done(((bf16[1,512,2752]{1,2,0:T(8,128)(2,1)}), bf16[1,4096,2752]{1,2,0:T(8,128)(2,1)}) %all-gather.43.cloned.1.call-update) | async-done | bytes 22544400 | tf_op jit(solution)/shard_map/all_gather | solution.py:73
  524.9 19.1 %multiply_convert_fusion.1.clone.4 = bf16[512,2752]{0,1:T(8,128)(2,1)S(1)} fusion(f32[512,2752]{0,1:T(8,128)} %fusion.12, bf16[512,4096]{1,0:T(8,128)(2,1)} %fusion.17, bf16[1,4096,2752]{1,2,0:T(8,128)(2,1)} %all-gather.43.cloned.1.call-done), kind=kOutput, calls=%fused_computation.67.clone.clone.clone.1 | convolution fusion | flops 11551178752 | bytes 35192832 | tf_op jit(solution)/shard_map/dot_general | solution.py:75
  544.0 90.4 %all-gather.45.cloned.1.call-done = bf16[1,2752,4096]{2,1,0:T(8,128)(2,1)} async-done(((bf16[1,2752,512]{2,1,0:T(8,128)(2,1)}), bf16[1,2752,4096]{2,1,0:T(8,128)(2,1)}) %all-gather.45.cloned.1.call-update) | async-done | bytes 22544400 | tf_op jit(solution)/shard_map/all_gather | solution.py:77
  634.4 18.4 %fusion.48 = bf16[512,4096]{1,0:T(8,128)(2,1)} fusion(bf16[1,2752,4096]{2,1,0:T(8,128)(2,1)} %all-gather.45.cloned.1.call-done, bf16[512,2752]{0,1:T(8,128)(2,1)S(1)} %multiply_convert_fusion.1.clone.4), kind=kOutput, calls=%fused_computation.62 | convolution fusion | flops 11544821760 | bytes 29556736 | tf_op jit(solution)/shard_map/dot_general | solution.py:78
  656.4 18.2 %all-gather.8 = f32[1,4096]{1,0:T(1,128)S(1)} all-gather(f32[1,512]{1,0:T(1,128)S(1)} %get-tuple-element.48), channel_id=10, replica_groups=mesh['dp'=1,'tp'=4,'fsdp'=8] {'fsdp'}, dimensions={1}, use_global_device_ids=true | all-gather | bytes 18432 | tf_op jit(solution)/shard_map/all_gather | solution.py:80
  674.6 66.0 %all-reduce.7.cloned.1.call-done = bf16[512,4096]{1,0:T(8,128)(2,1)} async-done(((bf16[512,4096]{1,0:T(8,128)(2,1)}), bf16[512,4096]{1,0:T(8,128)(2,1)}) %all-reduce.7.cloned.1.call-update) | async-done | bytes 4194320 | tf_op jit(solution)/shard_map/psum | solution.py:79
  744.1 6.4 fusion.21
  750.5 39.1 %all-gather.49.cloned.1.call-done = bf16[1,4096,1024]{2,1,0:T(8,128)(2,1)} async-done(((bf16[1,512,1024]{2,1,0:T(8,128)(2,1)}), bf16[1,4096,1024]{2,1,0:T(8,128)(2,1)}) %all-gather.49.cloned.1.call-update) | async-done | bytes 8388624 | tf_op jit(solution)/shard_map/all_gather | solution.py:55
  789.6 10.5 multiply_reduce_fusion.1
  800.0 38.4 %all-gather.51.cloned.1.call-done = bf16[1,4096,1024]{2,1,0:T(8,128)(2,1)} async-done(((bf16[1,512,1024]{2,1,0:T(8,128)(2,1)}), bf16[1,4096,1024]{2,1,0:T(8,128)(2,1)}) %all-gather.51.cloned.1.call-update) | async-done | bytes 8388624 | tf_op jit(solution)/shard_map/all_gather | solution.py:56
  838.4 10.5 multiply_reduce_fusion
  848.9 9.5 psum.45
  882.5 4.6 all-gather.47.cloned.1.call-done
  887.1 9.1 fusion.81
  905.0 5.5 fusion.136
  914.6 21.3 %all-gather.53.cloned.1.call-done = bf16[1,1024,4096]{2,1,0:T(8,128)(2,1)} async-done(((bf16[1,1024,512]{2,1,0:T(8,128)(2,1)}), bf16[1,1024,4096]{2,1,0:T(8,128)(2,1)}) %all-gather.53.cloned.1.call-update) | async-done | bytes 8388624 | tf_op jit(solution)/shard_map/all_gather | solution.py:67
  935.9 9.8 fusion.57
  947.8 17.3 %all-gather.13 = f32[1,4096]{1,0:T(1,128)S(1)} all-gather(f32[1,512]{1,0:T(1,128)S(1)} %copy-done.26), channel_id=15, replica_groups=mesh['dp'=1,'tp'=4,'fsdp'=8] {'fsdp'}, dimensions={1}, use_global_device_ids=true | all-gather | bytes 18432 | tf_op jit(solution)/shard_map/all_gather | solution.py:70
  965.1 67.9 %all-reduce.9.cloned.1.call-done = bf16[512,4096]{1,0:T(8,128)(2,1)} async-done(((bf16[512,4096]{1,0:T(8,128)(2,1)}), bf16[512,4096]{1,0:T(8,128)(2,1)}) %all-reduce.9.cloned.1.call-update) | async-done | bytes 4194320 | tf_op jit(solution)/shard_map/psum | solution.py:69
  1036.5 6.4 fusion.25
  1042.8 99.2 %all-gather.55.cloned.1.call-done = bf16[1,4096,2752]{1,2,0:T(8,128)(2,1)} async-done(((bf16[1,512,2752]{1,2,0:T(8,128)(2,1)}), bf16[1,4096,2752]{1,2,0:T(8,128)(2,1)}) %all-gather.55.cloned.1.call-update) | async-done | bytes 22544400 | tf_op jit(solution)/shard_map/all_gather | solution.py:72
  1142.1 19.0 %fusion.6 = f32[512,2752]{0,1:T(8,128)} fusion(bf16[512,4096]{1,0:T(8,128)(2,1)} %fusion.25, bf16[1,4096,2752]{1,2,0:T(8,128)(2,1)} %all-gather.55.cloned.1.call-done), kind=kOutput, calls=%fused_computation.6 | convolution fusion | flops 11542724608 | bytes 32374784 | tf_op jit(solution)/shard_map/dot_general | solution.py:74
  1161.1 90.3 %all-gather.57.cloned.1.call-done = bf16[1,4096,2752]{1,2,0:T(8,128)(2,1)} async-done(((bf16[1,512,2752]{1,2,0:T(8,128)(2,1)}), bf16[1,4096,2752]{1,2,0:T(8,128)(2,1)}) %all-gather.57.cloned.1.call-update) | async-done | bytes 22544400 | tf_op jit(solution)/shard_map/all_gather | solution.py:73
  1251.5 20.3 %multiply_convert_fusion.clone.2 = bf16[512,2752]{0,1:T(8,128)(2,1)} fusion(f32[512,2752]{0,1:T(8,128)} %fusion.6, bf16[512,4096]{1,0:T(8,128)(2,1)} %fusion.25, bf16[1,4096,2752]{1,2,0:T(8,128)(2,1)} %all-gather.57.cloned.1.call-done), kind=kOutput, calls=%fused_computation.66.clone.clone.clone | convolution fusion | flops 11551178752 | bytes 35192832 | tf_op jit(solution)/shard_map/dot_general | solution.py:75
  1271.7 89.1 %all-gather.59.cloned.1.call-done = bf16[1,2752,4096]{2,1,0:T(8,128)(2,1)} async-done(((bf16[1,2752,512]{2,1,0:T(8,128)(2,1)}), bf16[1,2752,4096]{2,1,0:T(8,128)(2,1)}) %all-gather.59.cloned.1.call-update) | async-done | bytes 22544400 | tf_op jit(solution)/shard_map/all_gather | solution.py:77
  1360.8 19.2 %fusion.51 = bf16[512,4096]{1,0:T(8,128)(2,1)} fusion(bf16[1,2752,4096]{2,1,0:T(8,128)(2,1)} %all-gather.59.cloned.1.call-done, bf16[512,2752]{0,1:T(8,128)(2,1)} %multiply_convert_fusion.clone.2), kind=kOutput, calls=%fused_computation.63 | convolution fusion | flops 11544821760 | bytes 29556736 | tf_op jit(solution)/shard_map/dot_general | solution.py:78
  1380.7 17.6 %all-gather.17 = f32[1,4096]{1,0:T(1,128)S(1)} all-gather(f32[1,512]{1,0:T(1,128)S(1)} %copy-done.27), channel_id=19, replica_groups=mesh['dp'=1,'tp'=4,'fsdp'=8] {'fsdp'}, dimensions={1}, use_global_device_ids=true | all-gather | bytes 18432 | tf_op jit(solution)/shard_map/all_gather | solution.py:80
  1406.8 61.2 %all-reduce.11.cloned.1.call-done = bf16[512,4096]{1,0:T(8,128)(2,1)} async-done(((bf16[512,4096]{1,0:T(8,128)(2,1)}), bf16[512,4096]{1,0:T(8,128)(2,1)}) %all-reduce.11.cloned.1.call-update) | async-done | bytes 4194320 | tf_op jit(solution)/shard_map/psum | solution.py:79
  1471.4 6.4 fusion.64
  (148 shorter events, 93.1 us)
Async XLA Ops:
  7.2 3.4 copy-start.15
  7.2 54.7 %all-gather.35.cloned.1.call-start = ((), (), s32[]{:S(2)}) async-start(), calls=%async_computation.5 | async-start | bytes 9437184 | tf_op jit(solution)/shard_map/all_gather | solution.py:55
  10.5 100.8 %all-gather.37.cloned.1.call-start = ((), (), s32[]{:S(2)}) async-start(), calls=%async_computation.6 | async-start | bytes 9437184 | tf_op jit(solution)/shard_map/all_gather | solution.py:56
  12.0 3.4 copy-start.16
  12.1 148.6 %all-gather.33.cloned.1.call-start = ((), (), s32[]{:S(2)}) async-start(), calls=%async_computation.4 | async-start | bytes 9437184 | tf_op jit(solution)/shard_map/all_gather | solution.py:57
  15.3 2.6 copy-start.24
  15.3 3.2 copy-start.25
  15.4 194.0 %all-gather.39.cloned.1.call-start = ((), (), s32[]{:S(2)}) async-start(), calls=%async_computation.7 | async-start | bytes 9437184 | tf_op jit(solution)/shard_map/all_gather | solution.py:67
  17.0 289.3 %all-reduce.5.cloned.1.call-start = ((), (), s32[]{:S(2)}) async-start(), calls=%async_computation | async-start | bytes 8388608 | tf_op jit(solution)/shard_map/psum | solution.py:69
  20.8 154.6 %copy-start.12 = (f32[512,64]{1,0:T(8,128)}, f32[512,64]{1,0:T(8,128)S(1)}, u32[]{:S(2)}) copy-start(f32[512,64]{1,0:T(8,128)S(1)} %get-tuple-element.55) | copy-start | bytes 393220
  131.1 1.6 copy-start.17
  169.9 5.4 copy-start.9
  171.7 3.6 copy-start.14
  177.0 1.0 copy-start.4
  177.0 1.3 copy-start.6
  178.3 1.4 copy-start.20
  179.7 5.5 copy-start.18
  219.0 196.3 %all-gather.41.cloned.1.call-start = ((), (), s32[]{:S(2)}) async-start(), calls=%async_computation.8 | async-start | bytes 25362432 | tf_op jit(solution)/shard_map/all_gather | solution.py:72
  224.6 300.2 %all-gather.43.cloned.1.call-start = ((), (), s32[]{:S(2)}) async-start(), calls=%async_computation.9 | async-start | bytes 25362432 | tf_op jit(solution)/shard_map/all_gather | solution.py:73
  230.2 5.6 copy-start.28
  230.2 404.2 %all-gather.45.cloned.1.call-start = ((), (), s32[]{:S(2)}) async-start(), calls=%async_computation.10 | async-start | bytes 25362432 | tf_op jit(solution)/shard_map/all_gather | solution.py:77
  235.7 504.9 %all-reduce.7.cloned.1.call-start = ((), (), s32[]{:S(2)}) async-start(), calls=%async_computation.1 | async-start | bytes 8388608 | tf_op jit(solution)/shard_map/psum | solution.py:79
  306.3 3.4 copy-start.1
  652.8 3.0 copy-start.29
  652.8 136.7 %all-gather.49.cloned.1.call-start = ((), (), s32[]{:S(2)}) async-start(), calls=%async_computation.12 | async-start | bytes 9437184 | tf_op jit(solution)/shard_map/all_gather | solution.py:55
  653.5 184.9 %all-gather.51.cloned.1.call-start = ((), (), s32[]{:S(2)}) async-start(), calls=%async_computation.13 | async-start | bytes 9437184 | tf_op jit(solution)/shard_map/all_gather | solution.py:56
  654.3 232.8 %all-gather.47.cloned.1.call-start = ((), (), s32[]{:S(2)}) async-start(), calls=%async_computation.11 | async-start | bytes 9437184 | tf_op jit(solution)/shard_map/all_gather | solution.py:57
  654.9 281.0 %all-gather.53.cloned.1.call-start = ((), (), s32[]{:S(2)}) async-start(), calls=%async_computation.14 | async-start | bytes 9437184 | tf_op jit(solution)/shard_map/all_gather | solution.py:67
  655.7 377.3 %all-reduce.9.cloned.1.call-start = ((), (), s32[]{:S(2)}) async-start(), calls=%async_computation.2 | async-start | bytes 8388608 | tf_op jit(solution)/shard_map/psum | solution.py:69
  740.7 3.4 copy-start
  800.0 58.4 %copy-start.23 = (f32[1,1024]{1,0:T(1,128)S(1)}, f32[1,1024]{1,0:T(1,128)}, u32[]{:S(2)}) copy-start(f32[1,1024]{1,0:T(1,128)} %get-tuple-element.45) | copy-start | bytes 12292
  864.8 3.8 copy-start.22
  882.5 16.1 %copy-start.13 = (f32[512,64]{1,0:T(8,128)S(1)}, f32[512,64]{1,0:T(8,128)}, u32[]{:S(2)}) copy-start(f32[512,64]{1,0:T(8,128)} %copy-done.12) | copy-start | bytes 393220
  896.3 1.0 copy-start.10
  902.6 1.0 copy-start.8
  903.6 1.4 copy-start.21
  905.0 5.5 copy-start.19
  945.7 196.3 %all-gather.55.cloned.1.call-start = ((), (), s32[]{:S(2)}) async-start(), calls=%async_computation.15 | async-start | bytes 25362432 | tf_op jit(solution)/shard_map/all_gather | solution.py:72
  945.8 1.9 copy-start.26
  946.4 305.1 %all-gather.57.cloned.1.call-start = ((), (), s32[]{:S(2)}) async-start(), calls=%async_computation.16 | async-start | bytes 25362432 | tf_op jit(solution)/shard_map/all_gather | solution.py:73
  947.0 413.8 %all-gather.59.cloned.1.call-start = ((), (), s32[]{:S(2)}) async-start(), calls=%async_computation.17 | async-start | bytes 25362432 | tf_op jit(solution)/shard_map/all_gather | solution.py:77
  947.7 520.3 %all-reduce.11.cloned.1.call-start = ((), (), s32[]{:S(2)}) async-start(), calls=%async_computation.3 | async-start | bytes 8388608 | tf_op jit(solution)/shard_map/psum | solution.py:79
  1033.0 3.4 copy-start.2
  1380.1 0.7 copy-start.27
  1380.1 19.8 %copy-start.5 = (bf16[1,512,8,64]{3,1,2,0:T(8,128)(2,1)S(1)}, bf16[1,512,8,64]{3,1,2,0:T(8,128)(2,1)}, u32[]{:S(2)}) copy-start(bf16[1,512,8,64]{3,1,2,0:T(8,128)(2,1)} %copy-done.4) | copy-start | bytes 1572868
  1380.1 19.8 %copy-start.7 = (bf16[1,512,8,64]{3,1,2,0:T(8,128)(2,1)S(1)}, bf16[1,512,8,64]{3,1,2,0:T(8,128)(2,1)}, u32[]{:S(2)}) copy-start(bf16[1,512,8,64]{3,1,2,0:T(8,128)(2,1)} %copy-done.6) | copy-start | bytes 1572868
  1399.9 5.2 copy-start.11
  1468.0 3.4 copy-start.3
Sparse Core Ops, SparseCore 0:
  10.6 51.2 all-gather.34
  64.1 47.1 all-gather.36
  113.5 47.1 all-gather.32
  162.2 47.1 all-gather.38
  219.1 87.1 all-reduce.4
  307.7 107.5 all-gather.40
  416.9 107.8 all-gather.42
  526.5 107.8 all-gather.44
  652.9 87.6 all-reduce.6
  742.1 47.3 all-gather.48
  791.2 47.1 all-gather.50
  839.9 47.1 all-gather.46
  888.7 47.1 all-gather.52
  945.9 87.1 all-reduce.8
  1034.5 107.5 all-gather.54
  1143.5 107.8 all-gather.56
  1252.9 107.8 all-gather.58
  1380.3 87.6 all-reduce.10
where the time goes:
time: 1490 us; the launch traced here: 1480 us
  waiting for transfers between devices  1040 us (70%)
  matrix products  203 us (14%)
  blocking collectives  90.1 us (6%)
  other arithmetic  67 us (4%)
  local copies, waits for them, and re-layouts  66 us (4%)
  between operations  14.9 us (1%)
    all_gather x2, waiting for transfers between devices, local_layers(): wg_full = lax.all_gather(w_gate[layer], 'fsdp', axis=0, tiled=True)  198 us
    all_gather x2, waiting for transfers between devices, local_layers(): wu_full = lax.all_gather(w_up[layer], 'fsdp', axis=0, tiled=True)  181 us
    all_gather x2, waiting for transfers between devices, local_layers(): wd_full = lax.all_gather(w_down[layer], 'fsdp', axis=1, tiled=True)  179 us
    psum x2, waiting for transfers between devices, local_layers(): m_out = lax.psum(m_part, 'tp').astype(jnp.float32)  127 us
    psum x2, waiting for transfers between devices, local_layers(): a_out = lax.psum(a_part, 'tp').astype(jnp.float32)  120 us
    all_gather x2, waiting for transfers between devices, local_layers(): wq_full = lax.all_gather(w_query[layer], 'fsdp', axis=0, tiled=True)  80.2 us
    all_gather x2, waiting for transfers between devices, local_layers(): wk_full = lax.all_gather(w_key[layer], 'fsdp', axis=0, tiled=True)  79.5 us
    all_gather x2, waiting for transfers between devices, local_layers(): wo_full = lax.all_gather(w_out[layer], 'fsdp', axis=1, tiled=True)  41.5 us
  transfers between devices with their start and end apart: 18, of which 18 were waited for; matrix products, arithmetic and copies ran while one was open for 18% of the time, Pallas kernels for 0%

commit v1 on v0

v1 whole, which is shorter than its diff:
```python
import jax
import jax.numpy as jnp
from jax import lax
from jax.experimental import pallas as pl
from jax.experimental.pallas import tpu as pltpu
from jax.sharding import PartitionSpec as P

HEAD_DIM = 128
NORM_EPS = 1e-6
ROPE_THETA = 500000.0
MESH = pl.DeviceIdType.MESH
BF16 = jnp.bfloat16
F32 = jnp.float32


def rope_tables(seq_len):
    half = HEAD_DIM // 2
    inv_freq = ROPE_THETA ** (-2.0 * jnp.arange(half, dtype=F32) / HEAD_DIM)
    angles = jnp.arange(seq_len, dtype=F32)[:, None] * inv_freq[None, :]
    cos_t, sin_t = jnp.cos(angles), jnp.sin(angles)
    return jnp.concatenate([cos_t, cos_t], axis=-1), jnp.concatenate([-sin_t, sin_t], axis=-1)


def layers_kernel(n_f, n_t, n_layers, *refs):
    (x_in, wq, wk, wv, wo, wg, wu, wd, gq, gk, gains, cos_ref, sin_ref) = refs[:13]
    y_out, k_out, v_out = refs[13:16]
    bufs = refs[16:16 + 5 * n_layers]
    (hid, acc_g, acc_u, kbuf, vbuf, obuf, act, part, full, r1, r2, sqbuf, gbuf,
     wb_qkv, wb_o, wb_gu, wb_d,
     unit_recv, unit_send, ld_sem, ar_recv, ar_send, sq_recv, sq_send, g_recv, g_send, io_sem) = refs[16 + 5 * n_layers:]

    f = lax.axis_index('fsdp')
    t = lax.axis_index('tp')
    tokens, width = hid.shape
    blk = width // n_f
    local_heads = kbuf.shape[1] // HEAD_DIM
    right = lax.rem(f + 2, n_f)
    left = lax.rem(f + n_f - 2, n_f)
    far = lax.rem(f + n_f // 2, n_f)
    mate = f + 1 - 2 * lax.rem(f, 2)
    t_a = t + 1 - 2 * lax.rem(t, 2)
    t_b = n_t - 1 - t
    key_a = lax.rem((t + 1) // 2, 2)
    key_b = t // 2

    barrier = pltpu.get_barrier_semaphore()
    for d in range(1, n_f):
        pl.semaphore_signal(barrier, inc=1, device_id={'fsdp': lax.rem(f + d, n_f)}, device_id_type=MESH)
    for d in range(1, n_t):
        pl.semaphore_signal(barrier, inc=1, device_id={'tp': lax.rem(t + d, n_t)}, device_id_type=MESH)
    pl.semaphore_wait(barrier, n_f + n_t - 2)

    def rcopy(src, dst, send_sem, recv_sem, dev):
        return pltpu.make_async_remote_copy(src_ref=src, dst_ref=dst, send_sem=send_sem, recv_sem=recv_sem,
                                            device_id=dev, device_id_type=MESH)

    units = []
    for layer in range(n_layers):
        b = bufs[5 * layer:5 * layer + 5]
        units.append((b[0], [wq.at[layer], wk.at[layer], wv.at[layer]]))
        units.append((b[1], [wo.at[layer]]))
        units.append((b[2], [wg.at[layer]]))
        units.append((b[3], [wu.at[layer]]))
        units.append((b[4], [wd.at[layer]]))
    n_units = len(units)

    def wait_bytes(ref, sem):
        pltpu.make_async_copy(ref, ref, sem).wait()

    def send_own(u):
        buf, srcs = units[u]
        for slot, dev in ((0, right), (1, left), (4, mate)):
            for j, src in enumerate(srcs):
                rcopy(src, buf.at[f, j], unit_send.at[u], unit_recv.at[u, slot], {'fsdp': dev}).start()

    def service(u):
        buf, srcs = units[u]
        half = buf.shape[2] // 2
        wait_bytes(buf.at[0], unit_recv.at[u, 0])
        src = buf.at[left, :, pl.ds(0, half)]
        rcopy(src, src, unit_send.at[u], unit_recv.at[u, 2], {'fsdp': right}).start()
        src = buf.at[left]
        rcopy(src, src, unit_send.at[u], unit_recv.at[u, 5], {'fsdp': mate}).start()
        wait_bytes(buf.at[0], unit_recv.at[u, 1])
        src = buf.at[right, :, pl.ds(half, half)]
        rcopy(src, src, unit_send.at[u], unit_recv.at[u, 3], {'fsdp': left}).start()
        src = buf.at[right]
        rcopy(src, src, unit_send.at[u], unit_recv.at[u, 6], {'fsdp': mate}).start()
        if u + 2 < n_units:
            send_own(u + 2)

    def finish(u):
        buf, srcs = units[u]
        half = buf.shape[2] // 2
        wait_bytes(buf.at[0, :, pl.ds(0, half)], unit_recv.at[u, 2])
        wait_bytes(buf.at[0, :, pl.ds(0, half)], unit_recv.at[u, 3])
        src = buf.at[far]
        rcopy(src, src, unit_send.at[u], unit_recv.at[u, 7], {'fsdp': mate}).start()
        for slot in (4, 5, 6, 7):
            wait_bytes(buf.at[0], unit_recv.at[u, slot])

    def stream(u, wb, body):
        buf, srcs = units[u]
        for j, src in enumerate(srcs):
            pltpu.make_async_copy(src, wb.at[0, j], ld_sem.at[0]).start()

        def step(i, carry):
            slot = lax.rem(i, 2)
            wait_bytes(wb.at[slot], ld_sem.at[slot])

            @pl.when(i < n_f - 1)
            def _():
                nxt = lax.rem(f + i + 1, n_f)
                pltpu.make_async_copy(buf.at[nxt], wb.at[1 - slot], ld_sem.at[1 - slot]).start()

            body(i, lax.rem(f + i, n_f), slot)
            return carry

        lax.fori_loop(0, n_f, step, 0)

    def accumulate(i, owner, wb, slot, j, acc, col0):
        n_cols = wb.shape[3]
        lhs = hid[:, pl.ds(pl.multiple_of(owner * blk, blk), blk)]
        tile = min(256, n_cols)

        def one(cols_w, cols_a):
            val = jnp.dot(lhs, wb[slot, j, :, cols_w], preferred_element_type=F32)

            @pl.when(i == 0)
            def _():
                acc[:, cols_a] = val

            @pl.when(i > 0)
            def _():
                acc[:, cols_a] += val

        def cols(n, carry):
            off = pl.multiple_of(n * tile, tile)
            one(pl.ds(off, tile), pl.ds(pl.multiple_of(col0 + off, 128), tile))
            return carry

        whole = n_cols // tile
        lax.fori_loop(0, whole, cols, 0)
        rest = n_cols - whole * tile
        if rest:
            one(pl.ds(whole * tile, rest), pl.ds(col0 + whole * tile, rest))

    rows = min(128, tokens)

    def by_rows(body):
        def step(i, carry):
            body(pl.ds(pl.multiple_of(i * rows, rows), rows))
            return carry

        lax.fori_loop(0, tokens // rows, step, 0)

    quarter = width // 4
    eighth = width // 8

    def tp_sum():
        def cols(start, size):
            return pl.ds(pl.multiple_of(start, eighth), size)

        def send(k, src, dst, dev):
            copy = rcopy(src, dst, ar_send.at[k], ar_recv.at[k], {'tp': dev})
            copy.start()
            return copy

        h2 = width // 2
        keep1, keep2 = key_a * quarter, h2 + key_b * quarter
        c0 = send(0, part.at[:, cols((1 - key_a) * quarter, quarter)], r1.at[0], t_a)
        c1 = send(1, part.at[:, cols(h2 + (1 - key_b) * quarter, quarter)], r1.at[1], t_b)

        def add(dst, dst_start, src_start, other, size):
            def body(rs):
                dst[rs, cols(dst_start, size)] = (part[rs, cols(src_start, size)].astype(F32)
                                                  + other[rs, :].astype(F32)).astype(BF16)
            by_rows(body)

        c0.wait_recv()
        add(part, keep1, keep1, r1.at[0], quarter)
        c2 = send(2, part.at[:, cols(keep1 + (1 - key_b) * eighth, eighth)], r2.at[0], t_b)
        c1.wait_recv()
        add(part, keep2, keep2, r1.at[1], quarter)
        c3 = send(3, part.at[:, cols(keep2 + (1 - key_a) * eighth, eighth)], r2.at[1], t_a)
        c2.wait_recv()
        fin1 = keep1 + key_b * eighth
        add(full, fin1, fin1, r2.at[0], eighth)
        c4 = send(4, full.at[:, cols(fin1, eighth)], full.at[:, cols(fin1, eighth)], t_b)
        c3.wait_recv()
        fin2 = keep2 + key_a * eighth
        add(full, fin2, fin2, r2.at[1], eighth)
        c5 = send(5, full.at[:, cols(fin2, eighth)], full.at[:, cols(fin2, eighth)], t_a)
        c4.wait_recv()
        c6 = send(6, full.at[:, cols(keep1, quarter)], full.at[:, cols(keep1, quarter)], t_a)
        c5.wait_recv()
        c7 = send(7, full.at[:, cols(keep2, quarter)], full.at[:, cols(keep2, quarter)], t_b)
        c6.wait_recv()
        c7.wait_recv()
        for c in (c0, c1, c2, c3, c4, c5, c6, c7):
            c.wait_send()

    nrows = min(32, tokens)

    def add_norm(row):
        def step(i, carry):
            rs = pl.ds(pl.multiple_of(i * nrows, nrows), nrows)
            vals = full[rs, :].astype(F32)
            scale = lax.rsqrt(jnp.sum(vals * vals, axis=-1, keepdims=True) / width + NORM_EPS)
            for s in range(n_f):
                cs = pl.ds(s * blk, blk)
                gain = gbuf[s, row:row + 1, :]
                hid[rs, cs] = (hid[rs, cs].astype(F32) + full[rs, cs].astype(F32) * scale * gain).astype(BF16)
            return carry

        lax.fori_loop(0, tokens // nrows, step, 0)

    def qkv_stage(layer, u):
        def body(i, owner, slot):
            accumulate(i, owner, wb_qkv, slot, 0, acc_g, 0)
            accumulate(i, owner, wb_qkv, slot, 1, acc_g, wb_qkv.shape[3])
            accumulate(i, owner, wb_qkv, slot, 2, acc_u, 0)

        stream(u, wb_qkv, body)

    def attention_stage(layer):
        hw = local_heads * HEAD_DIM
        first_half = lax.broadcasted_iota(jnp.int32, (rows, 128), 1) < 64

        def squares(rs):
            q_all = acc_g[rs, pl.ds(0, hw)]
            k_all = acc_g[rs, pl.ds(hw, hw)]
            sq = jnp.sum(q_all * q_all, axis=-1, keepdims=True)
            sk = jnp.sum(k_all * k_all, axis=-1, keepdims=True)
            sqbuf[layer, 0, rs, :] = jnp.where(first_half, sq, sk)

        by_rows(squares)
        copies = []
        for d in range(1, n_t):
            c = rcopy(sqbuf.at[layer, 0], sqbuf.at[layer, d], sq_send.at[layer, d - 1], sq_recv.at[layer, d - 1],
                      {'tp': lax.rem(t + d, n_t)})
            c.start()
            copies.append(c)
        for c in copies:
            c.wait_recv()
        for c in copies:
            c.wait_send()

        def total(rs):
            parts = [sqbuf[layer, lax.rem(t + n_t - dev, n_t), rs, :] for dev in range(n_t)]
            tot = parts[0]
            for p in parts[1:]:
                tot = tot + p
            sqbuf[layer, 0, rs, :] = lax.rsqrt(tot / width + NORM_EPS)

        by_rows(total)

        def head(h, carry):
            cs = pl.ds(pl.multiple_of(h * HEAD_DIM, HEAD_DIM), HEAD_DIM)
            ck = pl.ds(pl.multiple_of(hw + h * HEAD_DIM, HEAD_DIM), HEAD_DIM)
            cos_t, sin_t = cos_ref[...], sin_ref[...]

            def rope(v):
                return v * cos_t + pltpu.roll(v, HEAD_DIM // 2, 1) * sin_t

            inv = sqbuf[layer, 0, :, :]
            qh = rope(acc_g[:, cs] * inv[:, 0:1] * gq[layer:layer + 1, cs]).astype(BF16)
            kbuf[:, cs] = rope(acc_g[:, ck] * inv[:, 64:65] * gk[layer:layer + 1, cs]).astype(BF16)
            vbuf[:, cs] = acc_u[:, cs].astype(BF16)
            qb = min(256, tokens)
            for i in range(tokens // qb):
                end = (i + 1) * qb
                s = lax.dot_general(qh[i * qb:end], kbuf[0:end, cs], (((1,), (1,)), ((), ())),
                                    preferred_element_type=F32) * (HEAD_DIM ** -0.5)
                keep = (lax.broadcasted_iota(jnp.int32, (qb, end), 0) + i * qb
                        >= lax.broadcasted_iota(jnp.int32, (qb, end), 1))
                s = jnp.where(keep, s, -jnp.inf)
                e = jnp.exp(s - jnp.max(s, axis=-1, keepdims=True))
                p = (e / jnp.sum(e, axis=-1, keepdims=True)).astype(BF16)
                obuf[i * qb:end, cs] = jnp.dot(p, vbuf[0:end, cs], preferred_element_type=F32).astype(BF16)
            return carry

        lax.fori_loop(0, local_heads, head, 0)
        ck = pltpu.make_async_copy(kbuf, k_out.at[layer], io_sem.at[0])
        cv = pltpu.make_async_copy(vbuf, v_out.at[layer], io_sem.at[1])
        ck.start()
        cv.start()
        return ck, cv

    def wide_stage(u, lhs, wb):
        def body(i, owner, slot):
            val = jnp.dot(lhs[...], wb[slot, 0], preferred_element_type=F32)
            part[:, pl.ds(pl.multiple_of(owner * blk, blk), blk)] = val.astype(BF16)

        stream(u, wb, body)

    def act_stage():
        def body(rs):
            g = acc_g[rs, :]
            act[rs, :] = (g / (1.0 + jnp.exp(-g)) * acc_u[rs, :]).astype(BF16)

        by_rows(body)

    send_own(0)
    send_own(1)
    load_x = pltpu.make_async_copy(x_in, hid, io_sem.at[2])
    load_x.start()
    gbuf[f] = gains[...]
    for d in range(1, n_f):
        rcopy(gains, gbuf.at[f], g_send, g_recv, {'fsdp': lax.rem(f + d, n_f)}).start()
    load_x.wait()
    wait_bytes(gbuf.at[pl.ds(0, n_f - 1)], g_recv)
    wait_bytes(gbuf.at[pl.ds(0, n_f - 1)], g_send)
    service(0)

    def ready(u):
        if u + 1 < n_units:
            service(u + 1)
        finish(u)

    for layer in range(n_layers):
        u = 5 * layer
        ready(u)
        qkv_stage(layer, u)
        ck, cv = attention_stage(layer)
        ready(u + 1)
        wide_stage(u + 1, obuf, wb_o)
        tp_sum()
        add_norm(2 * layer)
        ck.wait()
        cv.wait()
        ready(u + 2)
        stream(u + 2, wb_gu, lambda i, owner, slot: accumulate(i, owner, wb_gu, slot, 0, acc_g, 0))
        ready(u + 3)
        stream(u + 3, wb_gu, lambda i, owner, slot: accumulate(i, owner, wb_gu, slot, 0, acc_u, 0))
        act_stage()
        ready(u + 4)
        wide_stage(u + 4, act, wb_d)
        tp_sum()
        add_norm(2 * layer + 1)

    store_y = pltpu.make_async_copy(hid, y_out, io_sem.at[2])
    store_y.start()
    for u in range(n_units):
        wait_bytes(units[u][0].at[pl.ds(0, 7)], unit_send.at[u])
    store_y.wait()


def solution(mesh):
    batch_axes = ('dp', 'fsdp')
    act_spec = P(batch_axes, None, None)
    in_cols = P(None, 'fsdp', 'tp')
    in_rows = P(None, 'tp', 'fsdp')
    tp_gain = P(None, 'tp')
    fsdp_gain = P(None, 'fsdp')
    cache_spec = P(None, batch_axes, None, 'tp', None)
    n_f, n_t = mesh.shape['fsdp'], mesh.shape['tp']

    def local_layers(x, w_query, w_key, w_value, w_out, w_gate, w_up, w_down, q_norm_w, k_norm_w, attn_norm_w, ffn_norm_w):
        batch, seq_len, width = x.shape
        n_layers, shard, hw = w_query.shape
        ff = w_gate.shape[2]
        tokens = batch * seq_len
        gains = jnp.stack([attn_norm_w, ffn_norm_w], axis=1).reshape(2 * n_layers, shard)
        gain_rows = -(-2 * n_layers // 8) * 8
        gains = jnp.pad(gains, ((0, gain_rows - 2 * n_layers), (0, 0)))
        cos_t, sin_t = rope_tables(seq_len)
        hbm = pl.BlockSpec(memory_space=pl.ANY)
        vmem = pl.BlockSpec(memory_space=pltpu.VMEM)
        layer_bufs = [jax.ShapeDtypeStruct((n_f, 3, shard, hw), BF16), jax.ShapeDtypeStruct((n_f, 1, hw, shard), BF16),
                      jax.ShapeDtypeStruct((n_f, 1, shard, ff), BF16), jax.ShapeDtypeStruct((n_f, 1, shard, ff), BF16),
                      jax.ShapeDtypeStruct((n_f, 1, ff, shard), BF16)]
        out_shape = [jax.ShapeDtypeStruct((tokens, width), BF16), jax.ShapeDtypeStruct((n_layers, tokens, hw), BF16),
                     jax.ShapeDtypeStruct((n_layers, tokens, hw), BF16)] + layer_bufs * n_layers
        scratch = [
            pltpu.VMEM((tokens, width), BF16),
            pltpu.VMEM((tokens, ff), F32),
            pltpu.VMEM((tokens, ff), F32),
            pltpu.VMEM((tokens, hw), BF16),
            pltpu.VMEM((tokens, hw), BF16),
            pltpu.VMEM((tokens, hw), BF16),
            pltpu.VMEM((tokens, ff), BF16),
            pltpu.VMEM((tokens, width), BF16),
            pltpu.VMEM((tokens, width), BF16),
            pltpu.VMEM((2, tokens, width // 4), BF16),
            pltpu.VMEM((2, tokens, width // 8), BF16),
            pltpu.VMEM((n_layers, n_t, tokens, 128), F32),
            pltpu.VMEM((n_f, gain_rows, shard), F32),
            pltpu.VMEM((2, 3, shard, hw), BF16),
            pltpu.VMEM((2, 1, hw, shard), BF16),
            pltpu.VMEM((2, 1, shard, ff), BF16),
            pltpu.VMEM((2, 1, ff, shard), BF16),
            pltpu.SemaphoreType.DMA((5 * n_layers, 8)),
            pltpu.SemaphoreType.DMA((5 * n_layers,)),
            pltpu.SemaphoreType.DMA((2,)),
            pltpu.SemaphoreType.DMA((8,)),
            pltpu.SemaphoreType.DMA((8,)),
            pltpu.SemaphoreType.DMA((n_layers, n_t - 1)),
            pltpu.SemaphoreType.DMA((n_layers, n_t - 1)),
            pltpu.SemaphoreType.DMA,
            pltpu.SemaphoreType.DMA,
            pltpu.SemaphoreType.DMA((3,)),
        ]
        outs = pl.pallas_call(
            lambda *refs: layers_kernel(n_f, n_t, n_layers, *refs),
            name='layers',
            out_shape=out_shape,
            in_specs=[hbm] * 8 + [vmem] * 5,
            out_specs=[hbm] * len(out_shape),
            scratch_shapes=scratch,
            compiler_params=pltpu.CompilerParams(collective_id=0, has_side_effects=True, vmem_limit_bytes=66 * 1000 * 1000),
        )(x.reshape(tokens, width), w_query, w_key, w_value, w_out, w_gate, w_up, w_down,
          q_norm_w, k_norm_w, gains, cos_t, sin_t)
        cache_shape = (n_layers, batch, seq_len, hw // HEAD_DIM, HEAD_DIM)
        return outs[0].reshape(batch, seq_len, width), outs[1].reshape(cache_shape), outs[2].reshape(cache_shape)

    return jax.shard_map(local_layers, mesh=mesh,
                         in_specs=(act_spec, in_cols, in_cols, in_cols, in_rows, in_cols, in_cols, in_rows,
                                   tp_gain, tp_gain, fsdp_gain, fsdp_gain),
                         out_specs=(act_spec, cache_spec, cache_spec), check_vma=False)
```

time: 1490 us -> 997 us (0.67)
  waiting for transfers between devices: 1040 us -> 0 us
  Pallas kernels: 0 us -> 965 us
  matrix products: 203 us -> 0 us
  blocking collectives: 90.1 us -> 0 us
  other arithmetic: 67 us -> 2.71 us
  local copies, waits for them, and re-layouts: 66 us -> 26.5 us
    pallas_call x0 -> x1, Pallas kernels: none -> 965 us  [local_layers(): pl.pallas_call(lambda *refs: layers_kernel(n_f, n_t, n_layers, *refs), na...]
    all_gather x14 -> x0, waiting for transfers between devices: 790 us -> none  [the longest x2 198 us: local_layers(): wg_full = lax.all_gather(w_gate[layer], 'fsdp', axis=0, tiled=True)]
    psum x4 -> x0, waiting for transfers between devices: 247 us -> none  [the longest x2 127 us: local_layers(): m_out = lax.psum(m_part, 'tp').astype(jnp.float32)]
    dot_general x18 -> x0, matrix products: 203 us -> none  [the longest x2 39.4 us: local_layers(): up_val = jnp.dot(h_new, wu_full, preferred_element_type=jnp.float32)]
    all_gather x4 -> x0, blocking collectives: 71.3 us -> none  [the longest x2 35.9 us: local_layers(): ffn_gain = lax.all_gather(ffn_norm_w[layer], 'fsdp', axis=0, tiled=True)]
    slice x16 -> x0, local copies, waits for them, and re-layouts: 37.1 us -> none  [the longest x2 5.51 us: apply_rope(): second = vals[..., half:]]
    convert_element_type x3 -> x0, other arithmetic: 19.1 us -> none  [the longest x2 12.7 us: local_layers(): (hidden.astype(jnp.float32) + a_out * rms_scale(a_out) * attn_gain).astyp...]
    psum x2 -> x0, blocking collectives: 18.8 us -> none  [local_layers(): sq_total = lax.psum(sq_local, 'tp')]
  transfers between devices with their start and end apart: 18 -> 0, of which waited for: 18 -> 0; matrix products, arithmetic and copies ran while one was open for 18% -> 0% of each run, Pallas kernels for 0% -> 0%
where the time goes in v1:
time: 997 us; the launch traced here: 995 us
  Pallas kernels  965 us (97%)
  local copies, waits for them, and re-layouts  26.5 us (3%)
    pallas_call x1, Pallas kernels, local_layers(): pl.pallas_call(lambda *refs: layers_kernel(n_f, n_t, n_layers, *refs), na...  965 us
    unnamed x7, local copies, waits for them, and re-layouts  25.9 us

profile of v1, /device:TPU:97, one launch (start us, length us, event | category | flops | bytes accessed | tf_op | source)
XLA Modules:
  0.0 995.1 jit_solution(17121873642487223370)
XLA Ops:
  0.6 0.7 pad_maximum_fusion.2
  1.4 0.6 pad.4.refs_10_
  2.0 1.0 fusion.2
  3.0 1.0 pad_maximum_fusion
  4.0 8.4 copy.16.refs_5_
  12.4 8.2 copy.17.refs_6_
  20.6 965.3 %layers.1 = (bf16[512,4096]{1,0:T(8,128)(2,1)}, bf16[2,512,1024]{2,1,0:T(8,128)(2,1)}, bf16[2,512,1024]{2,1,0:T(8,128)(2,1)}, bf16[8,3,512,1024]{3,2,1,0:T(8,128...) custom-call(bf16[512,4096]{1,0:T(8,128)(2,1)} %bitcast.19, ...), custom_call_target="tpu_custom_call" | custom-call | tf_op jit(solution)/shard_map/layers/pallas_call | solution.py:404
  985.9 0.0 copy-start
  985.9 3.7 copy.20
  989.6 3.5 copy.21
  993.1 0.0 copy-done
  993.1 2.0 copy.23
  (3 shorter events, 0.0 us)
Async XLA Ops:
  985.9 7.2 copy-start

commit v2 on v1

v2 whole, which is shorter than its diff:
```python
import jax
import jax.numpy as jnp
from jax import lax
from jax.experimental import pallas as pl
from jax.experimental.pallas import tpu as pltpu
from jax.sharding import PartitionSpec as P

HEAD_DIM = 128
NORM_EPS = 1e-6
ROPE_THETA = 500000.0
MESH = pl.DeviceIdType.MESH
BF16 = jnp.bfloat16
F32 = jnp.float32


def rope_tables(seq_len):
    half = HEAD_DIM // 2
    inv_freq = ROPE_THETA ** (-2.0 * jnp.arange(half, dtype=F32) / HEAD_DIM)
    angles = jnp.arange(seq_len, dtype=F32)[:, None] * inv_freq[None, :]
    cos_t, sin_t = jnp.cos(angles), jnp.sin(angles)
    return jnp.concatenate([cos_t, cos_t], axis=-1), jnp.concatenate([-sin_t, sin_t], axis=-1)


def layers_kernel(n_f, n_t, n_layers, *refs):
    (x_in, wq, wk, wv, wo, wg, wu, wd, gq, gk, gains, cos_ref, sin_ref) = refs[:13]
    y_out, k_out, v_out = refs[13:16]
    bufs = refs[16:16 + 5 * n_layers]
    (hid, acc_g, acc_u, kbuf, vbuf, obuf, act, part, full, r1, r2, pr, sqbuf, invbuf, gbuf,
     wb_qkv, wb_gu, wb_d,
     unit_recv, unit_send, ld_sem, ex_recv, ex_send, sq_recv, sq_send, g_recv, g_send, io_sem) = refs[16 + 5 * n_layers:]

    f = lax.axis_index('fsdp')
    t = lax.axis_index('tp')
    tokens, width = full.shape
    blk = width // n_f
    hw = kbuf.shape[1]
    local_heads = hw // HEAD_DIM
    ff_half = act.shape[1]
    own_rows, pair_rows = pl.ds(0, tokens), pl.ds(tokens, tokens)

    chip = f // 2
    core = lax.rem(f, 2)
    last_chip = n_f // 2 - 1
    mate = f + 1 - 2 * core
    near = f + 2 - 4 * lax.rem(chip, 2)
    pair = (last_chip - chip) * 2 + core
    near_pair = (last_chip - near // 2) * 2 + core
    cls = chip // 2
    t_a = t + 1 - 2 * lax.rem(t, 2)
    t_b = n_t - 1 - t
    key_a = lax.rem((t + 1) // 2, 2)
    key_b = t // 2

    barrier = pltpu.get_barrier_semaphore()
    for d in range(1, n_f):
        pl.semaphore_signal(barrier, inc=1, device_id={'fsdp': lax.rem(f + d, n_f)}, device_id_type=MESH)
    for d in range(1, n_t):
        pl.semaphore_signal(barrier, inc=1, device_id={'tp': lax.rem(t + d, n_t)}, device_id_type=MESH)
    pl.semaphore_wait(barrier, n_f + n_t - 2)

    def rcopy(src, dst, send_sem, recv_sem, dev):
        return pltpu.make_async_remote_copy(src_ref=src, dst_ref=dst, send_sem=send_sem, recv_sem=recv_sem,
                                            device_id=dev, device_id_type=MESH)

    def half_cols(which):
        return pl.ds(pl.multiple_of(which * ff_half, 128), ff_half)

    units = {}
    order = []
    for layer in range(n_layers):
        b = bufs[5 * layer:5 * layer + 5]
        units['q', layer] = (b[0], [wq.at[layer], wk.at[layer], wv.at[layer]], None)
        units['o', layer] = (b[1], [wo.at[layer]], None)
        units['g', layer] = (b[2], [wg.at[layer, :, half_cols(cls)]], wg.at[layer, :, half_cols(1 - cls)])
        units['u', layer] = (b[3], [wu.at[layer, :, half_cols(cls)]], wu.at[layer, :, half_cols(1 - cls)])
        units['d', layer] = (b[4], [wd.at[layer, half_cols(cls)]], wd.at[layer, half_cols(1 - cls)])
        first = ['q', 'o'] if layer == 0 else ['o', 'q']
        order += [(name, layer) for name in first + ['g', 'u', 'd']]
    n_units = len(order)
    place = {unit: i for i, unit in enumerate(order)}

    def wait_bytes(ref, sem):
        pltpu.make_async_copy(ref, ref, sem).wait()

    def send_own(u):
        buf, srcs, other = units[order[u]]
        for slot, dev in ((1, near), (0, pair), (4, mate)):
            for j, src in enumerate(srcs):
                if slot == 0 and other is not None:
                    src = other
                rcopy(src, buf.at[f, j], unit_send.at[u], unit_recv.at[u, slot], {'fsdp': dev}).start()

    def split(u):
        rows = units[order[u]][0].shape[2]
        if order[u][0] in ('g', 'u', 'd'):
            return rows
        return rows // 2 if u == 0 else rows // 8 * 3

    def pass_on(u, src, slot, dev):
        rcopy(src, src, unit_send.at[u], unit_recv.at[u, slot], {'fsdp': dev}).start()

    def service(unit):
        u = place[unit]
        buf = units[unit][0]
        rows, cut = buf.shape[2], split(u)
        wait_bytes(buf.at[0], unit_recv.at[u, 0])
        pass_on(u, buf.at[pair, :, pl.ds(0, cut)], 2, near)
        pass_on(u, buf.at[pair], 5, mate)
        wait_bytes(buf.at[0], unit_recv.at[u, 1])
        if cut < rows:
            pass_on(u, buf.at[near, :, pl.ds(cut, rows - cut)], 3, pair)
        pass_on(u, buf.at[near], 6, mate)
        if u + 2 < n_units:
            send_own(u + 2)

    def finish(unit):
        u = place[unit]
        buf = units[unit][0]
        rows, cut = buf.shape[2], split(u)
        wait_bytes(buf.at[0, :, pl.ds(0, cut)], unit_recv.at[u, 2])
        if cut < rows:
            wait_bytes(buf.at[0, :, pl.ds(cut, rows - cut)], unit_recv.at[u, 3])
        pass_on(u, buf.at[near_pair], 7, mate)
        for slot in (4, 5, 6, 7):
            wait_bytes(buf.at[0], unit_recv.at[u, slot])

    def stream(unit, wb, body):
        buf, srcs, _ = units[unit]
        for j, src in enumerate(srcs):
            pltpu.make_async_copy(src, wb.at[0, j], ld_sem.at[0]).start()

        def step(i, carry):
            slot = lax.rem(i, 2)
            wait_bytes(wb.at[slot], ld_sem.at[slot])

            @pl.when(i < n_f - 1)
            def _():
                nxt = lax.rem(f + i + 1, n_f)
                pltpu.make_async_copy(buf.at[nxt], wb.at[1 - slot], ld_sem.at[1 - slot]).start()

            body(i, lax.rem(f + i, n_f), slot)
            return carry

        lax.fori_loop(0, n_f, step, 0)

    def accumulate(i, owner, wb, slot, j, lhs_rows, acc, acc_rows):
        n_cols = wb.shape[3]
        lhs = hid[lhs_rows, pl.ds(pl.multiple_of(owner * blk, blk), blk)]
        tile = min(256, n_cols)

        def one(cols_w):
            val = jnp.dot(lhs, wb[slot, j, :, cols_w], preferred_element_type=F32)

            @pl.when(i == 0)
            def _():
                acc[acc_rows, cols_w] = val

            @pl.when(i > 0)
            def _():
                acc[acc_rows, cols_w] += val

        def cols(n, carry):
            one(pl.ds(pl.multiple_of(n * tile, tile), tile))
            return carry

        whole = n_cols // tile
        lax.fori_loop(0, whole, cols, 0)
        rest = n_cols - whole * tile
        if rest:
            one(pl.ds(whole * tile, rest))

    rows = min(128, tokens)

    def by_rows(body, total=tokens):
        def step(i, carry):
            body(i * rows)
            return carry

        lax.fori_loop(0, total // rows, step, 0)

    def chunk(start):
        return pl.ds(pl.multiple_of(start, rows), rows)

    quarter, eighth, half = width // 4, width // 8, width // 2
    keep1, keep2 = key_a * quarter, half + key_b * quarter
    fin1, fin2 = keep1 + key_b * eighth, keep2 + key_a * eighth

    def cols(start, size):
        return pl.ds(pl.multiple_of(start, eighth), size)

    def send(k, src, dst, dev):
        copy = rcopy(src, dst, ex_send.at[k], ex_recv.at[k], dev)
        copy.start()
        return copy

    def add(dst, dst_row0, row0, start, size, others):
        def body(r):
            val = part[chunk(row0 + r), cols(start, size)].astype(F32)
            for other in others:
                val = val + other[chunk(r), :].astype(F32)
            dst[chunk(dst_row0 + r), cols(start, size)] = val.astype(BF16)

        by_rows(body)

    def scatter_begin(g):
        rs = pl.ds(g * tokens, tokens)
        return [send(8 * g, part.at[rs, cols((1 - key_a) * quarter, quarter)], r1.at[2 * g], {'tp': t_a}),
                send(8 * g + 1, part.at[rs, cols(half + (1 - key_b) * quarter, quarter)], r1.at[2 * g + 1], {'tp': t_b})]

    def scatter_next(g, cs):
        rs, row0 = pl.ds(g * tokens, tokens), g * tokens
        cs[0].wait_recv()
        add(part, row0, row0, keep1, quarter, [r1.at[2 * g]])
        cs.append(send(8 * g + 2, part.at[rs, cols(keep1 + (1 - key_b) * eighth, eighth)], r2.at[2 * g], {'tp': t_b}))
        cs[1].wait_recv()
        add(part, row0, row0, keep2, quarter, [r1.at[2 * g + 1]])
        cs.append(send(8 * g + 3, part.at[rs, cols(keep2 + (1 - key_a) * eighth, eighth)], r2.at[2 * g + 1], {'tp': t_a}))

    def spread_first(k, buf, rs, which):
        start, dev = ((fin1, t_b), (fin2, t_a))[which]
        view = buf.at[rs, cols(start, eighth)]
        return send(k + which, view, view, {'tp': dev})

    def spread_next(k, buf, rs, cs):
        cs[0].wait_recv()
        view = buf.at[rs, cols(keep1, quarter)]
        cs.append(send(k + 2, view, view, {'tp': t_a}))
        cs[1].wait_recv()
        view = buf.at[rs, cols(keep2, quarter)]
        cs.append(send(k + 3, view, view, {'tp': t_b}))

    def drain(cs):
        for c in cs:
            c.wait_send()

    nrows = min(32, tokens)

    def add_norm(row):
        def step(i, carry):
            rs = pl.ds(pl.multiple_of(i * nrows, nrows), nrows)
            vals = full[rs, :].astype(F32)
            scale = lax.rsqrt(jnp.sum(vals * vals, axis=-1, keepdims=True) / width + NORM_EPS)
            for s in range(n_f):
                cs = pl.ds(s * blk, blk)
                gain = gbuf[s, row:row + 1, :]
                hid[rs, cs] = (hid[rs, cs].astype(F32) + full[rs, cs].astype(F32) * scale * gain).astype(BF16)
            return carry

        lax.fori_loop(0, tokens // nrows, step, 0)

    def qkv_stage(layer):
        def body(i, owner, slot):
            accumulate(i, owner, wb_qkv, slot, 0, own_rows, acc_g, own_rows)
            accumulate(i, owner, wb_qkv, slot, 1, own_rows, acc_g, pair_rows)
            accumulate(i, owner, wb_qkv, slot, 2, own_rows, acc_u, own_rows)

        stream(('q', layer), wb_qkv, body)

    n_blocks = tokens // 128

    def attention_stage(layer):
        lane = lax.broadcasted_iota(jnp.int32, (128, 128), 1)
        eye = lax.broadcasted_iota(jnp.int32, (128, 128), 0) == lane

        for which in range(2):
            for b in range(n_blocks):
                vals = acc_g[pl.ds(which * tokens + b * 128, 128), pl.ds(0, hw)]
                col = jnp.sum(vals * vals, axis=-1, keepdims=True)
                row = which * n_blocks + b
                sqbuf[layer, 0, row:row + 1, :] = jnp.sum(jnp.where(eye, col, 0.0), axis=0, keepdims=True)
        copies = []
        for d in range(1, n_t):
            c = rcopy(sqbuf.at[layer, 0], sqbuf.at[layer, d], sq_send.at[layer, d - 1], sq_recv.at[layer, d - 1],
                      {'tp': lax.rem(t + d, n_t)})
            c.start()
            copies.append(c)
        for c in copies:
            c.wait_recv()
        drain(copies)
        tot = sqbuf[layer, 0]
        for d in range(1, n_t):
            tot = tot + sqbuf[layer, d]
        inv_rows = lax.rsqrt(tot / width + NORM_EPS)
        for b in range(n_blocks):
            inv_q = jnp.sum(jnp.where(eye, inv_rows[b:b + 1, :], 0.0), axis=1, keepdims=True)
            inv_k = jnp.sum(jnp.where(eye, inv_rows[n_blocks + b:n_blocks + b + 1, :], 0.0), axis=1, keepdims=True)
            invbuf[pl.ds(b * 128, 128), :] = jnp.where(lane < 64, inv_q, inv_k)

        def head(h, carry):
            cs = pl.ds(pl.multiple_of(h * HEAD_DIM, HEAD_DIM), HEAD_DIM)
            cos_t, sin_t = cos_ref[...], sin_ref[...]

            def rope(v):
                return v * cos_t + pltpu.roll(v, HEAD_DIM // 2, 1) * sin_t

            inv = invbuf[...]
            qh = rope(acc_g[own_rows, cs] * inv[:, 0:1] * gq[layer:layer + 1, cs]).astype(BF16)
            kbuf[:, cs] = rope(acc_g[pair_rows, cs] * inv[:, 64:65] * gk[layer:layer + 1, cs]).astype(BF16)
            vbuf[:, cs] = acc_u[own_rows, cs].astype(BF16)
            qb = min(256, tokens)
            for i in range(tokens // qb):
                end = (i + 1) * qb
                s = lax.dot_general(qh[i * qb:end], kbuf[0:end, cs], (((1,), (1,)), ((), ())),
                                    preferred_element_type=F32) * (HEAD_DIM ** -0.5)
                keep = (lax.broadcasted_iota(jnp.int32, (qb, end), 0) + i * qb
                        >= lax.broadcasted_iota(jnp.int32, (qb, end), 1))
                s = jnp.where(keep, s, -jnp.inf)
                e = jnp.exp(s - jnp.max(s, axis=-1, keepdims=True))
                p = (e / jnp.sum(e, axis=-1, keepdims=True)).astype(BF16)
                obuf[i * qb:end, cs] = jnp.dot(p, vbuf[0:end, cs], preferred_element_type=F32).astype(BF16)
            return carry

        lax.fori_loop(0, local_heads, head, 0)
        ck = pltpu.make_async_copy(kbuf, k_out.at[layer], io_sem.at[0])
        cv = pltpu.make_async_copy(vbuf, v_out.at[layer], io_sem.at[1])
        ck.start()
        cv.start()
        return ck, cv

    def wide_stage(unit, lhs, out_rows, wb):
        def body(i, owner, slot):
            val = jnp.dot(lhs[...], wb[slot, 0], preferred_element_type=F32)
            part[out_rows, pl.ds(pl.multiple_of(owner * blk, blk), blk)] = val.astype(BF16)

        stream(unit, wb, body)

    def out_stage(layer):
        wide_stage(('o', layer), obuf, own_rows, wb_d.at[:, :, pl.ds(0, hw)])
        cs = scatter_begin(0)
        scatter_next(0, cs)
        cs[2].wait_recv()
        add(full, 0, 0, fin1, eighth, [r2.at[0]])
        cs2 = [spread_first(4, full, own_rows, 0)]
        cs[3].wait_recv()
        add(full, 0, 0, fin2, eighth, [r2.at[1]])
        cs2.append(spread_first(4, full, own_rows, 1))
        spread_next(4, full, own_rows, cs2)
        cs2[2].wait_recv()
        cs2[3].wait_recv()
        drain(cs + cs2)
        add_norm(2 * layer)

    def mlp_stage(layer):
        ex = []
        for k, start in ((16, fin1), (17, fin2)):
            ex.append(send(k, hid.at[own_rows, cols(start, eighth)], hid.at[pair_rows, cols(start, eighth)],
                           {'fsdp': pair}))

        def pass_over(name, acc, rs):
            stream((name, layer), wb_gu, lambda i, owner, slot: accumulate(i, owner, wb_gu, slot, 0, rs, acc, rs))

        service(('u', layer))
        finish(('g', layer))
        pass_over('g', acc_g, own_rows)
        ex[0].wait_recv()
        cs = [spread_first(12, hid, pair_rows, 0)]
        ex[1].wait_recv()
        cs.append(spread_first(12, hid, pair_rows, 1))
        service(('d', layer))
        spread_next(12, hid, pair_rows, cs)
        finish(('u', layer))
        pass_over('u', acc_u, own_rows)
        cs[2].wait_recv()
        cs[3].wait_recv()
        pass_over('g', acc_g, pair_rows)
        pass_over('u', acc_u, pair_rows)
        drain(ex + cs)

        def gate(r):
            g = acc_g[chunk(r), :]
            act[chunk(r), :] = (g / (1.0 + jnp.exp(-g)) * acc_u[chunk(r), :]).astype(BF16)

        by_rows(gate, 2 * tokens)

        finish(('d', layer))
        wide_stage(('d', layer), act, pl.ds(0, 2 * tokens), wb_d)
        cp = scatter_begin(1)
        co = scatter_begin(0)
        scatter_next(1, cp)
        scatter_next(0, co)
        cp[2].wait_recv()
        add(part, tokens, tokens, fin1, eighth, [r2.at[2]])
        ce = [send(18, part.at[pair_rows, cols(fin1, eighth)], pr.at[0], {'fsdp': pair})]
        cp[3].wait_recv()
        add(part, tokens, tokens, fin2, eighth, [r2.at[3]])
        ce.append(send(19, part.at[pair_rows, cols(fin2, eighth)], pr.at[1], {'fsdp': pair}))
        if layer + 1 < n_layers:
            service(('o', layer + 1))
        co[2].wait_recv()
        ce[0].wait_recv()
        add(full, 0, 0, fin1, eighth, [r2.at[0], pr.at[0]])
        cs = [spread_first(4, full, own_rows, 0)]
        co[3].wait_recv()
        ce[1].wait_recv()
        add(full, 0, 0, fin2, eighth, [r2.at[1], pr.at[1]])
        cs.append(spread_first(4, full, own_rows, 1))
        spread_next(4, full, own_rows, cs)
        if layer + 1 < n_layers:
            service(('q', layer + 1))
        cs[2].wait_recv()
        cs[3].wait_recv()
        drain(cp + co + ce + cs)
        add_norm(2 * layer + 1)

    send_own(0)
    send_own(1)
    load_x = pltpu.make_async_copy(x_in, hid.at[own_rows], io_sem.at[2])
    load_x.start()
    gbuf[f] = gains[...]
    for d in range(1, n_f):
        rcopy(gains, gbuf.at[f], g_send, g_recv, {'fsdp': lax.rem(f + d, n_f)}).start()
    load_x.wait()
    wait_bytes(gbuf.at[pl.ds(0, n_f - 1)], g_recv)
    wait_bytes(gbuf.at[pl.ds(0, n_f - 1)], g_send)
    service(('q', 0))
    service(('o', 0))

    for layer in range(n_layers):
        finish(('q', layer))
        qkv_stage(layer)
        ck, cv = attention_stage(layer)
        service(('g', layer))
        finish(('o', layer))
        out_stage(layer)
        ck.wait()
        cv.wait()
        mlp_stage(layer)

    store_y = pltpu.make_async_copy(hid.at[own_rows], y_out, io_sem.at[2])
    store_y.start()
    for u in range(n_units):
        wait_bytes(units[order[u]][0].at[pl.ds(0, 7)], unit_send.at[u])
    store_y.wait()


def solution(mesh):
    batch_axes = ('dp', 'fsdp')
    act_spec = P(batch_axes, None, None)
    in_cols = P(None, 'fsdp', 'tp')
    in_rows = P(None, 'tp', 'fsdp')
    tp_gain = P(None, 'tp')
    fsdp_gain = P(None, 'fsdp')
    cache_spec = P(None, batch_axes, None, 'tp', None)
    n_f, n_t = mesh.shape['fsdp'], mesh.shape['tp']

    def local_layers(x, w_query, w_key, w_value, w_out, w_gate, w_up, w_down, q_norm_w, k_norm_w, attn_norm_w, ffn_norm_w):
        batch, seq_len, width = x.shape
        n_layers, shard, hw = w_query.shape
        ff = w_gate.shape[2]
        tokens = batch * seq_len
        gains = jnp.stack([attn_norm_w, ffn_norm_w], axis=1).reshape(2 * n_layers, shard)
        gain_rows = -(-2 * n_layers // 8) * 8
        gains = jnp.pad(gains, ((0, gain_rows - 2 * n_layers), (0, 0)))
        cos_t, sin_t = rope_tables(seq_len)
        hbm = pl.BlockSpec(memory_space=pl.ANY)
        vmem = pl.BlockSpec(memory_space=pltpu.VMEM)
        ff_half = -(-ff // 256) * 128
        extra = 2 * ff_half - ff
        w_gate = jnp.pad(w_gate, ((0, 0), (0, 0), (0, extra)))
        w_up = jnp.pad(w_up, ((0, 0), (0, 0), (0, extra)))
        w_down = jnp.pad(w_down, ((0, 0), (0, extra), (0, 0)))
        layer_bufs = [jax.ShapeDtypeStruct((n_f, 3, shard, hw), BF16), jax.ShapeDtypeStruct((n_f, 1, hw, shard), BF16),
                      jax.ShapeDtypeStruct((n_f, 1, shard, ff_half), BF16),
                      jax.ShapeDtypeStruct((n_f, 1, shard, ff_half), BF16),
                      jax.ShapeDtypeStruct((n_f, 1, ff_half, shard), BF16)]
        out_shape = [jax.ShapeDtypeStruct((tokens, width), BF16), jax.ShapeDtypeStruct((n_layers, tokens, hw), BF16),
                     jax.ShapeDtypeStruct((n_layers, tokens, hw), BF16)] + layer_bufs * n_layers
        sq_rows = -(-2 * (tokens // 128) // 8) * 8
        scratch = [
            pltpu.VMEM((2 * tokens, width), BF16),
            pltpu.VMEM((2 * tokens, ff_half), F32),
            pltpu.VMEM((2 * tokens, ff_half), F32),
            pltpu.VMEM((tokens, hw), BF16),
            pltpu.VMEM((tokens, hw), BF16),
            pltpu.VMEM((tokens, hw), BF16),
            pltpu.VMEM((2 * tokens, ff_half), BF16),
            pltpu.VMEM((2 * tokens, width), BF16),
            pltpu.VMEM((tokens, width), BF16),
            pltpu.VMEM((4, tokens, width // 4), BF16),
            pltpu.VMEM((4, tokens, width // 8), BF16),
            pltpu.VMEM((2, tokens, width // 8), BF16),
            pltpu.VMEM((n_layers, n_t, sq_rows, 128), F32),
            pltpu.VMEM((tokens, 128), F32),
            pltpu.VMEM((n_f, gain_rows, shard), F32),
            pltpu.VMEM((2, 3, shard, hw), BF16),
            pltpu.VMEM((2, 1, shard, ff_half), BF16),
            pltpu.VMEM((2, 1, ff_half, shard), BF16),
            pltpu.SemaphoreType.DMA((5 * n_layers, 8)),
            pltpu.SemaphoreType.DMA((5 * n_layers,)),
            pltpu.SemaphoreType.DMA((2,)),
            pltpu.SemaphoreType.DMA((20,)),
            pltpu.SemaphoreType.DMA((20,)),
            pltpu.SemaphoreType.DMA((n_layers, n_t - 1)),
            pltpu.SemaphoreType.DMA((n_layers, n_t - 1)),
            pltpu.SemaphoreType.DMA,
            pltpu.SemaphoreType.DMA,
            pltpu.SemaphoreType.DMA((3,)),
        ]
        outs = pl.pallas_call(
            lambda *refs: layers_kernel(n_f, n_t, n_layers, *refs),
            name='layers',
            out_shape=out_shape,
            in_specs=[hbm] * 8 + [vmem] * 5,
            out_specs=[hbm] * len(out_shape),
            scratch_shapes=scratch,
            compiler_params=pltpu.CompilerParams(collective_id=0, has_side_effects=True, vmem_limit_bytes=66 * 1000 * 1000),
        )(x.reshape(tokens, width), w_query, w_key, w_value, w_out, w_gate, w_up, w_down,
          q_norm_w, k_norm_w, gains, cos_t, sin_t)
        cache_shape = (n_layers, batch, seq_len, hw // HEAD_DIM, HEAD_DIM)
        return outs[0].reshape(batch, seq_len, width), outs[1].reshape(cache_shape), outs[2].reshape(cache_shape)

    return jax.shard_map(local_layers, mesh=mesh,
                         in_specs=(act_spec, in_cols, in_cols, in_cols, in_rows, in_cols, in_cols, in_rows,
                                   tp_gain, tp_gain, fsdp_gain, fsdp_gain),
                         out_specs=(act_spec, cache_spec, cache_spec), check_vma=False)
```

time: 997 us -> 1020 us (1.023)
  local copies, waits for them, and re-layouts: 26.5 us -> 40.7 us
    pad x0 -> x3, local copies, waits for them, and re-layouts: none -> 14.1 us  [the longest x1 5.75 us: local_layers(): w_up = jnp.pad(w_up, ((0, 0), (0, 0), (0, extra)))]
    unnamed x7 -> x11, local copies, waits for them, and re-layouts: 25.9 us -> 26 us
where the time goes in v2:
time: 1020 us; the launch traced here: 1010 us
  Pallas kernels  968 us (95%)
  local copies, waits for them, and re-layouts  40.7 us (4%)
    pallas_call x1, Pallas kernels, local_layers(): pl.pallas_call(lambda *refs: layers_kernel(n_f, n_t, n_layers, *refs), na...  968 us
    unnamed x11, local copies, waits for them, and re-layouts  26 us

profile of v2, /device:TPU:97, one launch (start us, length us, event | category | flops | bytes accessed | tf_op | source)
XLA Modules:
  0.0 1011.7 jit_solution(1635166265549313199)
XLA Ops:
  0.6 0.7 pad_maximum_fusion.2
  1.4 0.6 pad.18.refs_10_
  2.0 1.0 fusion.2
  3.0 1.0 pad_maximum_fusion
  4.0 8.3 copy.15
  12.3 5.5 pad.15.refs_5_
  17.8 0.0 slice-start
  17.8 8.4 copy.16
  26.2 0.0 slice-start.1
  26.2 5.7 pad.16.refs_6_
  32.0 0.0 slice-done
  32.0 0.0 slice-done.1
  32.0 2.8 pad.17.refs_7_
  34.8 967.6 %layers.1 = (bf16[512,4096]{1,0:T(8,128)(2,1)}, bf16[2,512,1024]{2,1,0:T(8,128)(2,1)}, bf16[2,512,1024]{2,1,0:T(8,128)(2,1)}, bf16[8,3,512,1024]{3,2,1,0:T(8,128...) custom-call(bf16[512,4096]{1,0:T(8,128)(2,1)} %bitcast.21, ...), custom_call_target="tpu_custom_call" | custom-call | tf_op jit(solution)/shard_map/layers/pallas_call | solution.py:499
  1002.4 0.0 copy-start
  1002.5 3.7 copy.20
  1006.1 3.5 copy.21
  1009.7 0.0 copy-done
  1009.7 2.0 copy.23
  (4 shorter events, 0.0 us)
Async XLA Ops:
  17.8 14.2 %slice-start = ((s8[5636096]{0:T(1024)(128)(4,1)}), s8[1441792]{0:T(1024)(128)(4,1)S(1)}, s32[]{:S(2)}) async-start(s8[5636096]{0:T(1024)(128)(4,1)} %bitcast.18), calls=%async_computation | async-start | bytes 2883584
  26.2 5.8 slice-start.1
  1002.4 7.2 copy-start
